TPU v7x, 32 devices: a whole 2x2x4 slice. The times are simulated.
32 devices in a mesh: replica: 4 (over y, core), model: 8 (over z, x).
Axes of the slice: x: 2, y: 2, z: 4, core: 2. Of those that a mesh axis runs over, the one named last changes fastest.
Arguments:
- partial_query: float32 [4, 2048, 2048], P('replica', None, 'model'), may hold values from -4 to 4
- partial_key: float32 [4, 2048, 2048], P('replica', None, 'model'), may hold values from -4 to 4
- partial_value: float32 [4, 2048, 2048], P('replica', None, 'model'), may hold values from -4 to 4
- partial_mixed: float32 [4, 2048, 2048], P('replica', 'model'), may hold values from -4 to 4
- partial_norm: float32 [4, 2048], P('replica'), may hold values from -8 to 8
- partial_bias: float32 [4, 2048], P('replica'), may hold values from -8 to 8
- master_query: float32 [2048, 2048], P('replica', 'model'), may hold values from -0.1875 to 0.1875
- master_key: float32 [2048, 2048], P('replica', 'model'), may hold values from -0.1875 to 0.1875
- master_value: float32 [2048, 2048], P('replica', 'model'), may hold values from -0.1875 to 0.1875
- master_mixed: float32 [2048, 2048], P('model', 'replica'), may hold values from -0.1875 to 0.1875
- master_norm: float32 [2048], P('replica'), may hold values from 0.25 to 1.75
- master_bias: float32 [2048], P('replica'), may hold values from -3 to 3
- memory_query: float32 [2048, 2048], P('replica', 'model'), may hold values from 9.765625e-05 to 0.0009765625
- memory_key: float32 [2048, 2048], P('replica', 'model'), may hold values from 9.765625e-05 to 0.0009765625
- memory_value: float32 [2048, 2048], P('replica', 'model'), may hold values from 9.765625e-05 to 0.0009765625
- memory_mixed: float32 [2048, 2048], P('model', 'replica'), may hold values from 9.765625e-05 to 0.0009765625
- memory_norm: float32 [2048], P('replica'), may hold values from 0.05 to 0.8
- memory_bias: float32 [2048], P('replica'), may hold values from 0.05 to 0.8
Outputs:
- compute_query: bfloat16 [2048, 2048], P(None, 'model')
- compute_key: bfloat16 [2048, 2048], P(None, 'model')
- compute_value: bfloat16 [2048, 2048], P(None, 'model')
- compute_mixed: bfloat16 [2048, 2048], P('model')
- compute_norm: bfloat16 [2048], replicated
- compute_bias: bfloat16 [2048], replicated
- stepped_query: float32 [2048, 2048], P('replica', 'model')
- stepped_key: float32 [2048, 2048], P('replica', 'model')
- stepped_value: float32 [2048, 2048], P('replica', 'model')
- stepped_mixed: float32 [2048, 2048], P('model', 'replica')
- stepped_norm: float32 [2048], P('replica')
- stepped_bias: float32 [2048], P('replica')
- state_new_query: float32 [2048, 2048], P('replica', 'model')
- state_new_key: float32 [2048, 2048], P('replica', 'model')
- state_new_value: float32 [2048, 2048], P('replica', 'model')
- state_new_mixed: float32 [2048, 2048], P('model', 'replica')
- state_new_norm: float32 [2048], P('replica')
- state_new_bias: float32 [2048], P('replica')
All inputs are finite; a program needn't handle non-finite values.
Results may differ from a plain program's by a relative error of at most 0.0004.
Values may be sent and summed in bfloat16 or wider, within the bound.
A program may use at most 64 MiB of HBM per device.

v0:
```python
import jax
import jax.numpy as jnp
from jax import lax
from jax.sharding import PartitionSpec as P

learn_rate = 0.015
hold_rate = 0.8


def shards(
    partial_query,
    partial_key,
    partial_value,
    partial_mixed,
    partial_norm,
    partial_bias,
    master_query,
    master_key,
    master_value,
    master_mixed,
    master_norm,
    master_bias,
    memory_query,
    memory_key,
    memory_value,
    memory_mixed,
    memory_norm,
    memory_bias,
):
    mean_query, mean_key, mean_value, mean_mixed = (
        lax.psum_scatter(partial_query[0], "replica", scatter_dimension=0, tiled=True),
        lax.psum_scatter(partial_key[0], "replica", scatter_dimension=0, tiled=True),
        lax.psum_scatter(partial_value[0], "replica", scatter_dimension=0, tiled=True),
        lax.psum_scatter(partial_mixed[0], "replica", scatter_dimension=1, tiled=True),
    )
    whole_norm, whole_bias = lax.psum((partial_norm[0], partial_bias[0]), "replica")
    place = lax.axis_index("replica")
    mean_norm = lax.dynamic_slice_in_dim(
        whole_norm, place * master_norm.shape[0], master_norm.shape[0]
    )
    mean_bias = lax.dynamic_slice_in_dim(
        whole_bias, place * master_bias.shape[0], master_bias.shape[0]
    )
    mean_rate = lax.axis_size("replica") ** (-0.5)
    mean_query = mean_query * mean_rate
    mean_key = mean_key * mean_rate
    mean_value = mean_value * mean_rate
    mean_mixed = mean_mixed * mean_rate
    mean_norm = mean_norm * mean_rate
    mean_bias = mean_bias * mean_rate
    (
        own_query,
        own_key,
        own_value,
        own_mixed,
        slope_query_norm,
        slope_key_norm,
        slope_value_norm,
        slope_mixed_norm,
    ) = lax.psum(
        (
            jnp.sum(master_query * master_query, axis=1, keepdims=True),
            jnp.sum(master_key * master_key, axis=1, keepdims=True),
            jnp.sum(master_value * master_value, axis=1, keepdims=True),
            jnp.sum(master_mixed * master_mixed, axis=0, keepdims=True),
            jnp.sum(mean_query * mean_query, axis=1, keepdims=True),
            jnp.sum(mean_key * mean_key, axis=1, keepdims=True),
            jnp.sum(mean_value * mean_value, axis=1, keepdims=True),
            jnp.sum(mean_mixed * mean_mixed, axis=0, keepdims=True),
        ),
        "model",
    )
    mean_query = mean_query * (jnp.sqrt(own_query) * lax.rsqrt(slope_query_norm + 1e-06))
    mean_key = mean_key * (jnp.sqrt(own_key) * lax.rsqrt(slope_key_norm + 1e-06))
    mean_value = mean_value * (jnp.sqrt(own_value) * lax.rsqrt(slope_value_norm + 1e-06))
    mean_mixed = mean_mixed * (jnp.sqrt(own_mixed) * lax.rsqrt(slope_mixed_norm + 1e-06))
    state_new_query = hold_rate * memory_query + (1.0 - hold_rate) * mean_query * mean_query
    stepped_query = master_query - learn_rate * mean_query * lax.rsqrt(state_new_query + 1e-06)
    state_new_key = hold_rate * memory_key + (1.0 - hold_rate) * mean_key * mean_key
    stepped_key = master_key - learn_rate * mean_key * lax.rsqrt(state_new_key + 1e-06)
    state_new_value = hold_rate * memory_value + (1.0 - hold_rate) * mean_value * mean_value
    stepped_value = master_value - learn_rate * mean_value * lax.rsqrt(state_new_value + 1e-06)
    state_new_mixed = hold_rate * memory_mixed + (1.0 - hold_rate) * mean_mixed * mean_mixed
    stepped_mixed = master_mixed - learn_rate * mean_mixed * lax.rsqrt(state_new_mixed + 1e-06)
    state_new_norm = hold_rate * memory_norm + (1.0 - hold_rate) * mean_norm * mean_norm
    stepped_norm = master_norm - learn_rate * mean_norm * lax.rsqrt(state_new_norm + 1e-06)
    state_new_bias = hold_rate * memory_bias + (1.0 - hold_rate) * mean_bias * mean_bias
    stepped_bias = master_bias - learn_rate * mean_bias * lax.rsqrt(state_new_bias + 1e-06)
    compute_query, compute_key, compute_value, compute_mixed, compute_norm, compute_bias = (
        lax.all_gather(stepped_query.astype(jnp.bfloat16), "replica", axis=0, tiled=True),
        lax.all_gather(stepped_key.astype(jnp.bfloat16), "replica", axis=0, tiled=True),
        lax.all_gather(stepped_value.astype(jnp.bfloat16), "replica", axis=0, tiled=True),
        lax.all_gather(stepped_mixed.astype(jnp.bfloat16), "replica", axis=1, tiled=True),
        lax.all_gather(stepped_norm.astype(jnp.bfloat16), "replica", axis=0, tiled=True),
        lax.all_gather(stepped_bias.astype(jnp.bfloat16), "replica", axis=0, tiled=True),
    )
    return (
        compute_query,
        compute_key,
        compute_value,
        compute_mixed,
        compute_norm,
        compute_bias,
        stepped_query,
        stepped_key,
        stepped_value,
        stepped_mixed,
        stepped_norm,
        stepped_bias,
        state_new_query,
        state_new_key,
        state_new_value,
        state_new_mixed,
        state_new_norm,
        state_new_bias,
    )


def solution(mesh):
    in_specs = (
        P("replica", None, "model"),
        P("replica", None, "model"),
        P("replica", None, "model"),
        P("replica", "model", None),
        P("replica", None),
        P("replica", None),
        P("replica", "model"),
        P("replica", "model"),
        P("replica", "model"),
        P("model", "replica"),
        P("replica"),
        P("replica"),
        P("replica", "model"),
        P("replica", "model"),
        P("replica", "model"),
        P("model", "replica"),
        P("replica"),
        P("replica"),
    )
    out_specs = (
        P(None, "model"),
        P(None, "model"),
        P(None, "model"),
        P("model", None),
        P(),
        P(),
        P("replica", "model"),
        P("replica", "model"),
        P("replica", "model"),
        P("model", "replica"),
        P("replica"),
        P("replica"),
        P("replica", "model"),
        P("replica", "model"),
        P("replica", "model"),
        P("model", "replica"),
        P("replica"),
        P("replica"),
    )
    return jax.shard_map(shards, mesh=mesh, in_specs=in_specs, out_specs=out_specs, check_vma=False)
```

profile of v0, /device:TPU:0, one launch (start us, length us, event | category | flops | bytes accessed | tf_op | source)
XLA Modules:
  0.0 268.1 jit_solution(13964327610522615378)
XLA Ops:
  8.0 0.7 reduce-scatter.11.cloned.1.call-update
  10.8 33.6 %reduce-scatter.9.cloned.1.call-done = f32[512,256]{1,0:T(8,128)} async-done(((f32[2048,256]{1,0:T(8,128)}), f32[512,256]{1,0:T(8,128)}) %reduce-scatter.9.cloned.1.call-update) | async-done | bytes 524304 | tf_op jit(solution)/shard_map/reduce_scatter | solution.py:33
  44.5 1.2 multiply_reduce_fusion.2
  45.7 32.5 %reduce-scatter.11.cloned.1.call-done = f32[256,512]{1,0:T(8,128)} async-done(((f32[256,2048]{1,0:T(8,128)}), f32[256,512]{1,0:T(8,128)}) %reduce-scatter.11.cloned.1.call-update) | async-done | bytes 524304 | tf_op jit(solution)/shard_map/reduce_scatter | solution.py:34
  78.2 1.1 multiply_reduce_fusion
  79.3 32.6 %reduce-scatter.5.cloned.1.call-done = f32[512,256]{1,0:T(8,128)} async-done(((f32[2048,256]{1,0:T(8,128)}), f32[512,256]{1,0:T(8,128)}) %reduce-scatter.5.cloned.1.call-update) | async-done | bytes 524304 | tf_op jit(solution)/shard_map/reduce_scatter | solution.py:31
  112.0 1.2 multiply_reduce_fusion.6
  113.2 32.4 %reduce-scatter.7.cloned.1.call-done = f32[512,256]{1,0:T(8,128)} async-done(((f32[2048,256]{1,0:T(8,128)}), f32[512,256]{1,0:T(8,128)}) %reduce-scatter.7.cloned.1.call-update) | async-done | bytes 524304 | tf_op jit(solution)/shard_map/reduce_scatter | solution.py:32
  145.6 1.2 multiply_reduce_fusion.4
  146.7 37.1 %all-reduce = (f32[512,1]{0,1:T(1,128)S(1)}, f32[512,1]{0,1:T(1,128)S(1)}, f32[512,1]{0,1:T(1,128)S(1)}, f32[512,1]{0,1:T(1,128)S(1)}, f32[512,1]{0,1:T(1,128)S(...) all-reduce(f32[512,1]{0,1:T(1,128)S(1)} %bitcast.38, ...), channel_id=1, replica_groups=mesh['replica'=4,'model'=8] {'model'}, use_global_device_ids=true, to_apply=%region_4.0 | all-reduce | flops 4096 | bytes 32768 | tf_op jit(solution)/shard_map/psum | solution.py:60
  183.9 2.3 fusion.10
  186.3 2.4 fusion.8
  188.8 1.2 fusion.6
  190.2 1.3 fusion.12
  191.5 10.8 %all-reduce.1 = (f32[2048]{0:T(1024)S(1)}, f32[2048]{0:T(1024)S(1)}) all-reduce(f32[2048]{0:T(1024)S(1)} %bitcast.40, f32[2048]{0:T(1024)S(1)} %bitcast.41), channel_id=1, replica_groups=mesh['replica'=4,'model'=8] {'replica'}, use_global_device_ids=true, to_apply=%region_20.0 | all-reduce | flops 4096 | bytes 32768 | tf_op jit(solution)/shard_map/psum | solution.py:36
  203.0 5.2 %all-gather = bf16[4,1,512]{2,1,0:T(2,128)(2,1)S(1)} all-gather(bf16[1,1,512]{2,1,0:T(2,128)(2,1)S(1)} %reshape.44), channel_id=1, replica_groups=mesh['replica'=4,'model'=8] {'replica'}, dimensions={0}, use_global_device_ids=true | all-gather | bytes 5120 | tf_op jit(solution)/shard_map/all_gather | solution.py:94
  208.8 5.3 %all-gather.1 = bf16[4,1,512]{2,1,0:T(2,128)(2,1)S(1)} all-gather(bf16[1,1,512]{2,1,0:T(2,128)(2,1)S(1)} %reshape.46), channel_id=1, replica_groups=mesh['replica'=4,'model'=8] {'replica'}, dimensions={0}, use_global_device_ids=true | all-gather | bytes 5120 | tf_op jit(solution)/shard_map/all_gather | solution.py:95
  214.8 3.6 %all-gather.11.cloned.1.call-done = bf16[2048,256]{1,0:T(8,128)(2,1)} async-done(((bf16[512,256]{1,0:T(8,128)(2,1)}), bf16[2048,256]{1,0:T(8,128)(2,1)}) %all-gather.11.cloned.1.call-update) | async-done | bytes 1048592 | tf_op jit(solution)/shard_map/all_gather | solution.py:92
  218.3 18.8 %all-gather.13.cloned.1.call-done = bf16[256,2048]{1,0:T(8,128)(2,1)} async-done(((bf16[256,512]{1,0:T(8,128)(2,1)}), bf16[256,2048]{1,0:T(8,128)(2,1)}) %all-gather.13.cloned.1.call-update) | async-done | bytes 1048592 | tf_op jit(solution)/shard_map/all_gather | solution.py:93
  237.2 18.9 %all-gather.7.cloned.1.call-done = bf16[2048,256]{1,0:T(8,128)(2,1)} async-done(((bf16[512,256]{1,0:T(8,128)(2,1)}), bf16[2048,256]{1,0:T(8,128)(2,1)}) %all-gather.7.cloned.1.call-update) | async-done | bytes 1048592 | tf_op jit(solution)/shard_map/all_gather | solution.py:90
  256.0 2.4 copy.42
  258.4 1.0 copy.43
  259.4 1.0 copy.44
  260.3 1.0 copy.45
  (68 shorter events, 5.1 us)
Async XLA Ops:
  7.2 37.3 %reduce-scatter.9.cloned.1.call-start = ((), (), s32[]{:S(2)}) async-start(), calls=%async_computation.8 | async-start | bytes 2621440 | tf_op jit(solution)/shard_map/reduce_scatter | solution.py:33
  7.9 70.3 %reduce-scatter.11.cloned.1.call-start = ((), (), s32[]{:S(2)}) async-start(), calls=%async_computation.10 | async-start | bytes 2621440 | tf_op jit(solution)/shard_map/reduce_scatter | solution.py:34
  8.7 103.3 %reduce-scatter.5.cloned.1.call-start = ((), (), s32[]{:S(2)}) async-start(), calls=%async_computation.4 | async-start | bytes 2621440 | tf_op jit(solution)/shard_map/reduce_scatter | solution.py:31
  8.7 1.5 copy-start.2
  9.4 136.1 %reduce-scatter.7.cloned.1.call-start = ((), (), s32[]{:S(2)}) async-start(), calls=%async_computation.6 | async-start | bytes 2621440 | tf_op jit(solution)/shard_map/reduce_scatter | solution.py:32
  10.0 173.8 %copy-start.10 = (f32[512,256]{1,0:T(8,128)S(1)}, f32[512,256]{1,0:T(8,128)}, u32[]{:S(2)}) copy-start(f32[512,256]{1,0:T(8,128)} %param.31) | copy-start | bytes 1572868
  10.0 204.8 %all-gather.9.cloned.1.call-start = ((), (), s32[]{:S(2)}) async-start(), calls=%async_computation.7 | async-start | bytes 1310720 | tf_op jit(solution)/shard_map/all_gather | solution.py:91
  79.3 106.9 %copy-start.6 = (f32[512,256]{1,0:T(8,128)S(1)}, f32[512,256]{1,0:T(8,128)}, u32[]{:S(2)}) copy-start(f32[512,256]{1,0:T(8,128)} %reduce-scatter.9.cloned.1.call-done) | copy-start | bytes 1572868
  186.2 2.6 copy-start.5
  186.2 2.6 copy-start.11
  186.2 32.1 %all-gather.11.cloned.1.call-start = ((), (), s32[]{:S(2)}) async-start(), calls=%async_computation.9 | async-start | bytes 1310720 | tf_op jit(solution)/shard_map/all_gather | solution.py:92
  188.7 1.5 copy-start.4
  188.7 1.5 copy-start.12
  188.7 48.5 %all-gather.13.cloned.1.call-start = ((), (), s32[]{:S(2)}) async-start(), calls=%async_computation.11 | async-start | bytes 1310720 | tf_op jit(solution)/shard_map/all_gather | solution.py:93
  190.0 1.5 copy-start.13
  190.0 1.5 copy-start.14
  190.0 12.3 %copy-start.15 = (f32[512]{0:T(512)S(1)}, f32[512]{0:T(512)}, u32[]{:S(2)}) copy-start(f32[512]{0:T(512)} %param.29) | copy-start | bytes 6148
  190.0 12.3 %copy-start.16 = (f32[512]{0:T(512)S(1)}, f32[512]{0:T(512)}, u32[]{:S(2)}) copy-start(f32[512]{0:T(512)} %param.35) | copy-start | bytes 6148
  190.0 12.3 %copy-start.17 = (f32[512]{0:T(512)S(1)}, f32[512]{0:T(512)}, u32[]{:S(2)}) copy-start(f32[512]{0:T(512)} %param.28) | copy-start | bytes 6148
  190.1 12.3 %copy-start.18 = (f32[512]{0:T(512)S(1)}, f32[512]{0:T(512)}, u32[]{:S(2)}) copy-start(f32[512]{0:T(512)} %param.34) | copy-start | bytes 6148
  190.1 65.9 %all-gather.7.cloned.1.call-start = ((), (), s32[]{:S(2)}) async-start(), calls=%async_computation.5 | async-start | bytes 1310720 | tf_op jit(solution)/shard_map/all_gather | solution.py:90
  214.8 43.6 %copy-start.7 = (bf16[2048,256]{1,0:T(8,128)(2,1)S(1)}, bf16[2048,256]{1,0:T(8,128)(2,1)}, u32[]{:S(2)}) copy-start(bf16[2048,256]{1,0:T(8,128)(2,1)} %all-gather.9.cloned.1.call-done) | copy-start | bytes 3145732
  256.0 3.3 %copy-start.8 = (bf16[2048,256]{1,0:T(8,128)(2,1)S(1)}, bf16[2048,256]{1,0:T(8,128)(2,1)}, u32[]{:S(2)}) copy-start(bf16[2048,256]{1,0:T(8,128)(2,1)} %all-gather.11.cloned.1.call-done) | copy-start | bytes 3145732
  258.4 1.9 copy-start.9
  (3 other events, 3.7 us)
Sparse Core Ops, SparseCore 0:
  10.5 33.9 reduce-scatter.8
  47.0 31.1 reduce-scatter.10
  80.7 31.1 reduce-scatter.4
  114.3 31.1 reduce-scatter.6
  186.3 13.1 all-gather.8
  201.5 16.7 all-gather.10
  220.5 16.6 all-gather.12
  239.3 16.6 all-gather.6
where the time goes:
time: 269 us; the launch traced here: 268 us
  waiting for transfers between devices  175 us (65%)
  blocking collectives  58.4 us (22%)
  between operations  14.4 us (5%)
  other arithmetic  13.2 us (5%)
  local copies, waits for them, and re-layouts  6.78 us (3%)
    psum x1, blocking collectives, shards(): lax.psum((jnp.sum(master_query * master_query, axis=1, keepdims=True), jn...  37.1 us
    reduce_scatter x1, waiting for transfers between devices, shards(): lax.psum_scatter(partial_value[0], 'replica', scatter_dimension=0, tiled=...  33.6 us
    reduce_scatter x1, waiting for transfers between devices, shards(): lax.psum_scatter(partial_query[0], 'replica', scatter_dimension=0, tiled=...  32.6 us
    reduce_scatter x1, waiting for transfers between devices, shards(): lax.psum_scatter(partial_mixed[0], 'replica', scatter_dimension=1, tiled=...  32.5 us
    reduce_scatter x1, waiting for transfers between devices, shards(): lax.psum_scatter(partial_key[0], 'replica', scatter_dimension=0, tiled=True)  32.4 us
    all_gather x1, waiting for transfers between devices, shards(): lax.all_gather(stepped_query.astype(jnp.bfloat16), 'replica', axis=0, til...  18.9 us
    all_gather x1, waiting for transfers between devices, shards(): lax.all_gather(stepped_mixed.astype(jnp.bfloat16), 'replica', axis=1, til...  18.8 us
    psum x1, blocking collectives, shards(): lax.psum((partial_norm[0], partial_bias[0]), 'replica')  10.8 us
  transfers between devices with their start and end apart: 8, of which 7 were waited for; matrix products, arithmetic and copies ran while one was open for 4% of the time, Pallas kernels for 0%

commit v1 on v0

v1 whole, which is shorter than its diff:
```python
import functools

import jax
import jax.numpy as jnp
from jax import lax
from jax.experimental import pallas as pl
from jax.experimental.pallas import tpu as pltpu
from jax.sharding import PartitionSpec as P

learn_rate = 0.015
hold_rate = 0.8
CORES = 2
AXES = (0, 0, 0, 1)


def cut(ref, axis, start, size):
    where = pl.ds(pl.multiple_of(start, 128), size)
    return ref.at[where, :] if axis == 0 else ref.at[:, where]


def update(mean, master, memory):
    state = hold_rate * memory + (1.0 - hold_rate) * mean * mean
    return master - learn_rate * mean * lax.rsqrt(state + 1e-06), state


def kernel(replicas, models, length, width, *refs):
    n = len(AXES)
    partial, vec_partial = refs[0:4], refs[4:6]
    master_in, vec_master = refs[6:10], refs[10:12]
    memory_in, vec_memory = refs[12:16], refs[16:18]
    compute_out, vec_compute = refs[18:22], refs[22:24]
    stepped_out, vec_stepped = refs[24:28], refs[28:30]
    state_out, vec_state = refs[30:34], refs[34:36]
    (own_r, own_c, sib_r, sib_c, rem_r, rem_c, mas_r, mas_c, mem_r, mem_c, comp_r, comp_c,
     far_r, far_c, near_r, near_c, squares, ratios, norms,
     vpart, vfull, vcomp,
     load_sem, near_send, near_recv, far_send, far_recv, norm_send, norm_recv,
     ag_send, ag_recv, sib_send, sib_recv, out_sem, vload_sem, vsend_sem, vrecv_sem, vout_sem) = refs[36:]
    chips = replicas // CORES
    place = lax.axis_index("replica")
    part = lax.axis_index("model")
    chip, core = place // CORES, place % CORES
    sibling = chip * CORES + (CORES - 1 - core)
    rate = replicas ** (-0.5)

    def at(row_ref, col_ref, i, *index):
        return row_ref.at[(i,) + index] if AXES[i] == 0 else col_ref.at[index]

    def to_replica(r):
        return {"replica": r, "model": part}

    def to_model(m):
        return {"replica": place, "model": m}

    def remote(src, dst, send, recv, device):
        return pltpu.make_async_remote_copy(
            src_ref=src, dst_ref=dst, send_sem=send, recv_sem=recv,
            device_id=device, device_id_type=pl.DeviceIdType.MESH)

    def chip_at(d):
        return lax.rem(chip + d, chips)

    order = list(range(1, chips)) + [0]
    loads = {}
    for i in range(n):
        for d in order:
            loads[i, d] = pltpu.make_async_copy(
                cut(partial[i].at[0], AXES[i], (chip_at(d) * CORES + core) * length, length),
                at(own_r, own_c, i, d), load_sem.at[i, d])
            loads[i, d].start()
    for i in range(n):
        for name, src, rows, cols, k in (("master", master_in, mas_r, mas_c, 0), ("memory", memory_in, mem_r, mem_c, 1)):
            loads[i, name] = pltpu.make_async_copy(src[i], at(rows, cols, i), load_sem.at[i, chips + k])
            loads[i, name].start()

    barrier = pltpu.get_barrier_semaphore()
    for d in range(1, replicas):
        pl.semaphore_signal(barrier, inc=1, device_id=to_replica(lax.rem(place + d, replicas)),
                            device_id_type=pl.DeviceIdType.MESH)
    for d in range(1, models):
        pl.semaphore_signal(barrier, inc=1, device_id=to_model(lax.rem(part + d, models)),
                            device_id_type=pl.DeviceIdType.MESH)
    pl.semaphore_wait(barrier, replicas - 1 + models - 1)

    near = {}
    for i in range(n):
        for d in order:
            near[i, d] = remote(
                cut(partial[i].at[0], AXES[i], (chip_at(d) * CORES + (CORES - 1 - core)) * length, length),
                at(sib_r, sib_c, i, d), near_send.at[i, d], near_recv.at[i, d], to_replica(sibling))
            near[i, d].start()

    mine = pl.ds(pl.multiple_of(place * length, 128), length)
    vsrc = [vec_partial[0], vec_partial[1], vec_master[0], vec_master[1], vec_memory[0], vec_memory[1]]
    vcopies = []
    for d in range(replicas):
        for k in range(6):
            dst = vpart.at[k, d] if k < 2 else vfull.at[k - 2, :, mine]
            if d == 0:
                c = pltpu.make_async_copy(vsrc[k], dst, vload_sem.at[k])
            else:
                c = remote(vsrc[k], dst, vsend_sem.at[d - 1, k], vrecv_sem.at[d - 1, k],
                           to_replica(lax.rem(place + d, replicas)))
            c.start()
            vcopies.append(c)

    def step_rows(i):
        return 64 if AXES[i] == 0 else 32

    def each(i, body, init=None):
        rows = length if AXES[i] == 0 else width
        step = step_rows(i)

        def run(j, carry):
            return body(pl.ds(pl.multiple_of(j * step, step), step), carry)

        return lax.fori_loop(0, rows // step, run, init)

    def add_sibling(i, d):
        loads[i, d].wait()
        near[i, d].wait_recv()
        own, sib = at(own_r, own_c, i, d), at(sib_r, sib_c, i, d)

        def body(rows, carry):
            own[rows, :] = own[rows, :] + sib[rows, :]
            return carry

        each(i, body, 0)

    far = {}
    for i in range(n):
        for d in range(1, chips):
            add_sibling(i, d)
            far[i, d] = remote(
                at(own_r, own_c, i, d), at(rem_r, rem_c, i, d - 1), far_send.at[i, d - 1], far_recv.at[i, d - 1],
                to_replica(chip_at(d) * CORES + core))
            far[i, d].start()

    lanes = lax.broadcasted_iota(jnp.int32, (64, 128), 1)
    for i in range(n):
        add_sibling(i, 0)
        loads[i, "master"].wait()
        loads[i, "memory"].wait()
        master = at(mas_r, mas_c, i)
        if AXES[i] == 0:
            def body(rows, carry, master=master, i=i):
                v = master[rows, :]
                squares[i, rows, :] = jnp.broadcast_to(jnp.sum(v * v, axis=1, keepdims=True), (64, 128))
                return carry

            each(i, body, 0)
        else:
            def body(rows, carry, master=master):
                v = master[rows, :]
                return carry + jnp.sum(v * v, axis=0, keepdims=True)

            own_mixed = each(i, body, jnp.zeros((1, length), jnp.float32))
            norms[i, 0] = jnp.broadcast_to(own_mixed, (8, length))

    for c in vcopies:
        c.wait()
    vouts = []
    for k in range(2):
        total = vpart[k, 0]
        for d in range(1, replicas):
            total = total + vpart[k, d]
        stepped, state = update(total * rate, vfull[k], vfull[2 + k])
        vfull[k] = stepped
        vfull[2 + k] = state
        vcomp[k] = stepped.astype(jnp.bfloat16)
        vouts.append(pltpu.make_async_copy(vcomp.at[k], vec_compute[k], vout_sem.at[k]))
        vouts.append(pltpu.make_async_copy(vfull.at[k, :, mine], vec_stepped[k], vout_sem.at[2 + k]))
        vouts.append(pltpu.make_async_copy(vfull.at[2 + k, :, mine], vec_state[k], vout_sem.at[4 + k]))
    for c in vouts:
        c.start()

    outs = list(vouts)
    sends = []
    gather, give = {}, {}
    for i in range(n):
        for d in range(1, chips):
            far[i, d].wait_recv()
        own = at(own_r, own_c, i, 0)
        rem = [at(rem_r, rem_c, i, d) for d in range(chips - 1)]

        def mean_of(rows, own=own, rem=rem):
            total = own[rows, :]
            for r in rem:
                total = total + r[rows, :]
            total = total * rate
            own[rows, :] = total
            return total

        if AXES[i] == 0:
            def body(rows, carry, i=i, mean_of=mean_of):
                v = mean_of(rows)
                slope = jnp.broadcast_to(jnp.sum(v * v, axis=1, keepdims=True), (64, 128))
                squares[i, rows, :] = jnp.where(lanes == 1, slope, squares[i, rows, :])
                return carry

            each(i, body, 0)
            norms[i, 0] = squares[i].T[0:8]
        else:
            def body(rows, carry, mean_of=mean_of):
                v = mean_of(rows)
                return carry + jnp.sum(v * v, axis=0, keepdims=True)

            slope = each(i, body, jnp.zeros((1, length), jnp.float32))
            row = lax.broadcasted_iota(jnp.int32, (8, length), 0)
            norms[i, 0] = jnp.where(row == 1, jnp.broadcast_to(slope, (8, length)), norms[i, 0])
        passed = []
        for d in range(1, models):
            c = remote(norms.at[i, 0], norms.at[i, d], norm_send.at[i, d - 1], norm_recv.at[i, d - 1],
                       to_model(lax.rem(part + d, models)))
            c.start()
            passed.append(c)
        for c in passed:
            c.wait_recv()
        total = norms[i, 0]
        for d in range(1, models):
            total = total + norms[i, d]
        ratio = jnp.sqrt(total[0:1]) * lax.rsqrt(total[1:2] + 1e-06)
        for c in passed:
            c.wait_send()
        if AXES[i] == 0:
            ratios[i] = jnp.broadcast_to(ratio, (128, length)).T

        master, memory, comp = at(mas_r, mas_c, i), at(mem_r, mem_c, i), at(comp_r, comp_c, i)

        def body(rows, carry, i=i, ratio=ratio, own=own, master=master, memory=memory, comp=comp):
            scale = ratios[i, rows, 0:1] if AXES[i] == 0 else ratio
            stepped, state = update(own[rows, :] * scale, master[rows, :], memory[rows, :])
            master[rows, :] = stepped
            memory[rows, :] = state
            comp[rows, :] = stepped.astype(jnp.bfloat16)
            return carry

        each(i, body, 0)
        for d in range(1, chips):
            gather[i, d] = remote(comp, at(far_r, far_c, i, d - 1), ag_send.at[i, d - 1], ag_recv.at[i, d - 1],
                                  to_replica(chip_at(d) * CORES + core))
            gather[i, d].start()
        give[i, 0] = remote(comp, at(near_r, near_c, i, 0), sib_send.at[i, 0], sib_recv.at[i, 0], to_replica(sibling))
        give[i, 0].start()
        for k, c in enumerate((
                pltpu.make_async_copy(comp, cut(compute_out[i], AXES[i], place * length, length), out_sem.at[i, 0]),
                pltpu.make_async_copy(master, stepped_out[i], out_sem.at[i, 1]),
                pltpu.make_async_copy(memory, state_out[i], out_sem.at[i, 2]))):
            c.start()
            outs.append(c)

    def write(i, buffer, r, k):
        c = pltpu.make_async_copy(buffer, cut(compute_out[i], AXES[i], r * length, length), out_sem.at[i, k])
        c.start()
        outs.append(c)

    for i in range(n):
        for d in range(1, chips):
            gather[i, d].wait_recv()
            buffer = at(far_r, far_c, i, d - 1)
            give[i, d] = remote(buffer, at(near_r, near_c, i, d), sib_send.at[i, d], sib_recv.at[i, d], to_replica(sibling))
            give[i, d].start()
            write(i, buffer, chip_at(chips - d) * CORES + core, 2 + d)
        give[i, 0].wait_recv()
        write(i, at(near_r, near_c, i, 0), sibling, 2 + chips)
    for i in range(n):
        for d in range(1, chips):
            give[i, d].wait_recv()
            write(i, at(near_r, near_c, i, d), chip_at(chips - d) * CORES + (CORES - 1 - core), 2 + chips + d)
    for group in (near, far, gather, give):
        for c in group.values():
            c.wait_send()
    for c in outs:
        c.wait()


def shards(*args):
    replicas, models = lax.axis_size("replica"), lax.axis_size("model")
    chips = replicas // CORES
    args = list(args)
    for k in (10, 11, 16, 17):
        args[k] = args[k].reshape(1, -1)
    length, width = args[6].shape
    n, rows = len(AXES), sum(a == 0 for a in AXES)
    f32, bf16 = jnp.float32, jnp.bfloat16
    total = length * replicas
    row, col = (length, width), (width, length)
    outs = []
    for a in AXES:
        outs.append(jax.ShapeDtypeStruct((total, width) if a == 0 else (width, total), bf16))
    outs += [jax.ShapeDtypeStruct((1, total), bf16)] * 2
    one = [jax.ShapeDtypeStruct(row if a == 0 else col, f32) for a in AXES]
    one += [jax.ShapeDtypeStruct((1, length), f32)] * 2
    outs += one + one
    dma = pltpu.SemaphoreType.DMA
    scratch = []
    for lead, kind in ((chips, f32), (chips, f32), (chips - 1, f32), (None, f32), (None, f32), (None, bf16),
                       (chips - 1, bf16), (chips, bf16)):
        more = () if lead is None else (lead,)
        scratch += [pltpu.VMEM((rows,) + more + row, kind), pltpu.VMEM(more + col, kind)]
    scratch += [
        pltpu.VMEM((rows, length, 128), f32),
        pltpu.VMEM((rows, length, 128), f32),
        pltpu.VMEM((n, models, 8, length), f32),
        pltpu.VMEM((2, replicas, 1, total), f32),
        pltpu.VMEM((4, 1, total), f32),
        pltpu.VMEM((2, 1, total), bf16),
        dma((n, chips + 2)), dma((n, chips)), dma((n, chips)), dma((n, chips - 1)), dma((n, chips - 1)),
        dma((n, models - 1)), dma((n, models - 1)),
        dma((n, chips - 1)), dma((n, chips - 1)), dma((n, chips)), dma((n, chips)),
        dma((n, 2 + 2 * chips)), dma((6,)), dma((replicas - 1, 6)), dma((replicas - 1, 6)), dma((6,)),
    ]
    anywhere = pl.BlockSpec(memory_space=pl.ANY)
    result = pl.pallas_call(
        functools.partial(kernel, replicas, models, length, width),
        out_shape=outs,
        in_specs=[anywhere] * len(args),
        out_specs=[anywhere] * len(outs),
        scratch_shapes=scratch,
        compiler_params=pltpu.CompilerParams(collective_id=0, has_side_effects=True),
    )(*args)
    result = list(result)
    for k in (4, 5, 10, 11, 16, 17):
        result[k] = result[k].reshape(-1)
    return tuple(result)


def solution(mesh):
    ins = [P("replica", None, "model")] * 3 + [P("replica", "model", None)] + [P("replica", None)] * 2
    held = [P("replica", "model")] * 3 + [P("model", "replica")] + [P("replica")] * 2
    whole = [P(None, "model")] * 3 + [P("model", None)] + [P()] * 2
    return jax.shard_map(shards, mesh=mesh, in_specs=tuple(ins + held + held),
                         out_specs=tuple(whole + held + held), check_vma=False)
```

time: 269 us -> 98.9 us (0.37)
  waiting for transfers between devices: 175 us -> 0 us
  Pallas kernels: 0 us -> 81.2 us
  blocking collectives: 58.4 us -> 0 us
  between operations: 14.4 us -> 0.71 us
  other arithmetic: 13.2 us -> 2.72 us
  local copies, waits for them, and re-layouts: 6.78 us -> 14 us
    reduce_scatter x4 -> x0, waiting for transfers between devices: 131 us -> none  [the longest x1 33.6 us: shards(): lax.psum_scatter(partial_value[0], 'replica', scatter_dimension=0, tiled=...]
    pallas_call x0 -> x1, Pallas kernels: none -> 81.2 us  [shards(): pl.pallas_call(functools.partial(kernel, replicas, models, length, width)...]
    psum x2 -> x0, blocking collectives: 47.8 us -> none  [the longest x1 37.1 us: shards(): lax.psum((jnp.sum(master_query * master_query, axis=1, keepdims=True), jn...]
    all_gather x4 -> x0, waiting for transfers between devices: 41.2 us -> none  [the longest x1 18.9 us: shards(): lax.all_gather(stepped_query.astype(jnp.bfloat16), 'replica', axis=0, til...]
    all_gather x2 -> x0, blocking collectives: 10.5 us -> none  [the longest x1 5.33 us: shards(): lax.all_gather(stepped_bias.astype(jnp.bfloat16), 'replica', axis=0, tile...]
    convert_element_type x5 -> x0, other arithmetic: 7.94 us -> none  [the longest x1 2.4 us: shards(): stepped_value.astype(jnp.bfloat16)]
    unnamed x46, local copies, waits for them, and re-layouts: 6.78 us -> 14 us
    reduce_sum x8 -> x0, other arithmetic: 5.19 us -> none  [the longest x1 1.19 us: shards(): jnp.sum(mean_query * mean_query, axis=1, keepdims=True)]
  transfers between devices with their start and end apart: 8 -> 0, of which waited for: 7 -> 0; matrix products, arithmetic and copies ran while one was open for 4% -> 0% of each run, Pallas kernels for 0% -> 0%
where the time goes in v1:
time: 98.9 us; the launch traced here: 98.6 us
  Pallas kernels  81.2 us (82%)
  local copies, waits for them, and re-layouts  14 us (14%)
  other arithmetic  2.72 us (3%)
    pallas_call x1, Pallas kernels, shards(): pl.pallas_call(functools.partial(kernel, replicas, models, length, width)...  81.2 us
    unnamed x46, local copies, waits for them, and re-layouts  14 us
    pallas_call x2, other arithmetic, shards(): pl.pallas_call(functools.partial(kernel, replicas, models, length, width)...  2.72 us

profile of v1, /device:TPU:0, one launch (start us, length us, event | category | flops | bytes accessed | tf_op | source)
XLA Modules:
  0.0 98.6 jit_solution(16037470531729637311)
XLA Ops:
  0.7 81.2 %shard_map.313 = (bf16[2048,256]{1,0:T(8,128)(2,1)}, bf16[2048,256]{1,0:T(8,128)(2,1)}, bf16[2048,256]{1,0:T(8,128)(2,1)}, bf16[256,2048]{1,0:T(8,128)(2,1)}, bf...) custom-call(f32[1,2048,256]{2,1,0:T(8,128)} %refs_0_.1, ...), custom_call_target="tpu_custom_call" | custom-call | tf_op jit(solution)/shard_map/pallas_call | solution.py:314
  81.9 0.0 copy-start.2
  81.9 1.4 %reduce = bf16[2048]{0:T(1024)(128)(2,1)} reduce(bf16[1,2048]{1,0:T(2,128)(2,1)} %get-tuple-element.40, bf16[]{:T(256)} %constant.6), dimensions={0}, to_apply=%get-tuple-element.40.reduce_sub_computation | reduce | bytes 8194 | tf_op jit(solution)/shard_map/pallas_call | solution.py:314
  83.3 1.3 %reduce.1 = bf16[2048]{0:T(1024)(128)(2,1)} reduce(bf16[1,2048]{1,0:T(2,128)(2,1)} %get-tuple-element.41, bf16[]{:T(256)} %constant.6), dimensions={0}, to_apply=%get-tuple-element.41.reduce_sub_computation | reduce | bytes 8194 | tf_op jit(solution)/shard_map/pallas_call | solution.py:314
  84.6 2.4 %copy.52 = bf16[2048,256]{1,0:T(8,128)(2,1)} copy(bf16[2048,256]{1,0:T(8,128)(2,1)} %get-tuple-element.72) | data formatting | bytes 2097152
  87.0 0.0 copy-done.2
  87.0 1.0 copy.53
  88.0 1.0 copy.54
  88.9 1.0 copy.55
  89.9 0.0 copy-done.10
  89.9 0.8 copy.56
  90.7 0.8 copy.57
  91.5 0.8 copy.58
  92.3 0.8 copy.59
  93.1 0.6 copy.60
  93.7 0.0 copy-done.13
  93.7 0.6 copy.61
  94.3 0.8 copy.62
  95.1 0.8 copy.63
  95.9 0.8 copy.64
  96.7 0.8 copy.65
  97.5 0.0 copy-done.12
  97.5 0.6 copy.66
  98.1 0.6 copy.67
  (25 shorter events, 0.0 us)
Async XLA Ops:
  81.9 5.1 %copy-start.2 = (bf16[2048,256]{1,0:T(8,128)(2,1)S(1)}, bf16[2048,256]{1,0:T(8,128)(2,1)}, u32[]{:S(2)}) copy-start(bf16[2048,256]{1,0:T(8,128)(2,1)} %get-tuple-element.73) | copy-start | bytes 3145732
  84.6 3.3 %copy-start.1 = (bf16[2048,256]{1,0:T(8,128)(2,1)S(1)}, bf16[2048,256]{1,0:T(8,128)(2,1)}, u32[]{:S(2)}) copy-start(bf16[2048,256]{1,0:T(8,128)(2,1)} %get-tuple-element.74) | copy-start | bytes 3145732
  87.0 1.9 %copy-start = (bf16[256,2048]{1,0:T(8,128)(2,1)S(1)}, bf16[256,2048]{1,0:T(8,128)(2,1)}, u32[]{:S(2)}) copy-start(bf16[256,2048]{1,0:T(8,128)(2,1)} %get-tuple-element.75) | copy-start | bytes 3145732
  88.0 2.0 %copy-start.10 = (f32[512,256]{1,0:T(8,128)S(1)}, f32[512,256]{1,0:T(8,128)}, u32[]{:S(2)}) copy-start(f32[512,256]{1,0:T(8,128)} %get-tuple-element.78) | copy-start | bytes 1572868
  88.9 1.8 %copy-start.9 = (f32[512,256]{1,0:T(8,128)S(1)}, f32[512,256]{1,0:T(8,128)}, u32[]{:S(2)}) copy-start(f32[512,256]{1,0:T(8,128)} %get-tuple-element.79) | copy-start | bytes 1572868
  88.9 2.6 %copy-start.8 = (f32[512,256]{1,0:T(8,128)S(1)}, f32[512,256]{1,0:T(8,128)}, u32[]{:S(2)}) copy-start(f32[512,256]{1,0:T(8,128)} %get-tuple-element.80) | copy-start | bytes 1572868
  89.9 2.4 %copy-start.7 = (f32[256,512]{1,0:T(8,128)S(1)}, f32[256,512]{1,0:T(8,128)}, u32[]{:S(2)}) copy-start(f32[256,512]{1,0:T(8,128)} %get-tuple-element.81) | copy-start | bytes 1572868
  89.9 3.2 %copy-start.14 = (f32[1,512]{1,0:T(1,128)S(1)}, f32[1,512]{1,0:T(1,128)}, u32[]{:S(2)}) copy-start(f32[1,512]{1,0:T(1,128)} %get-tuple-element.46) | copy-start | bytes 6148
  89.9 3.8 %copy-start.13 = (f32[1,512]{1,0:T(1,128)S(1)}, f32[1,512]{1,0:T(1,128)}, u32[]{:S(2)}) copy-start(f32[1,512]{1,0:T(1,128)} %get-tuple-element.47) | copy-start | bytes 6148
  89.9 4.4 %copy-start.6 = (f32[512,256]{1,0:T(8,128)S(1)}, f32[512,256]{1,0:T(8,128)}, u32[]{:S(2)}) copy-start(f32[512,256]{1,0:T(8,128)} %get-tuple-element.84) | copy-start | bytes 1572868
  90.7 4.4 %copy-start.5 = (f32[512,256]{1,0:T(8,128)S(1)}, f32[512,256]{1,0:T(8,128)}, u32[]{:S(2)}) copy-start(f32[512,256]{1,0:T(8,128)} %get-tuple-element.85) | copy-start | bytes 1572868
  91.5 4.4 %copy-start.4 = (f32[512,256]{1,0:T(8,128)S(1)}, f32[512,256]{1,0:T(8,128)}, u32[]{:S(2)}) copy-start(f32[512,256]{1,0:T(8,128)} %get-tuple-element.86) | copy-start | bytes 1572868
  92.3 4.4 %copy-start.3 = (f32[256,512]{1,0:T(8,128)S(1)}, f32[256,512]{1,0:T(8,128)}, u32[]{:S(2)}) copy-start(f32[256,512]{1,0:T(8,128)} %get-tuple-element.87) | copy-start | bytes 1572868
  94.3 3.2 %copy-start.12 = (f32[1,512]{1,0:T(1,128)S(1)}, f32[1,512]{1,0:T(1,128)}, u32[]{:S(2)}) copy-start(f32[1,512]{1,0:T(1,128)} %get-tuple-element.52) | copy-start | bytes 6148
  94.3 3.8 %copy-start.11 = (f32[1,512]{1,0:T(1,128)S(1)}, f32[1,512]{1,0:T(1,128)}, u32[]{:S(2)}) copy-start(f32[1,512]{1,0:T(1,128)} %get-tuple-element.53) | copy-start | bytes 6148

commit v2 on v1

--- a/solution.py
+++ b/solution.py
@@ -16,6 +16,23 @@
 def cut(ref, axis, start, size):
     where = pl.ds(pl.multiple_of(start, 128), size)
     return ref.at[where, :] if axis == 0 else ref.at[:, where]
+
+
+REACH = 4.0
+SCALE = 2.0**15 / (CORES * REACH)
+
+
+def encode(x):
+    t = x * SCALE
+    square = t * t
+    return (square * square * square * (t * jnp.abs(t))).astype(jnp.bfloat16)
+
+
+def decode(y):
+    y = y.astype(jnp.float32)
+    fourth = lax.rsqrt(lax.rsqrt(jnp.maximum(jnp.abs(y), 2.0**-126)))
+    root = fourth * lax.rsqrt(fourth) * (1.0 / SCALE)
+    return jnp.where(y > 0.0, root, jnp.where(y < 0.0, -root, 0.0))
 
 
 def update(mean, master, memory):
@@ -31,9 +48,9 @@
     compute_out, vec_compute = refs[18:22], refs[22:24]
     stepped_out, vec_stepped = refs[24:28], refs[28:30]
     state_out, vec_state = refs[30:34], refs[34:36]
-    (own_r, own_c, sib_r, sib_c, rem_r, rem_c, mas_r, mas_c, mem_r, mem_c, comp_r, comp_c,
+    (own_r, own_c, sib_r, sib_c, code_r, code_c, rem_r, rem_c, full_r, full_c, mas_r, mas_c, mem_r, mem_c, comp_r, comp_c,
      far_r, far_c, near_r, near_c, squares, ratios, norms,
-     vpart, vfull, vcomp,
+     vpart, vfull,
      load_sem, near_send, near_recv, far_send, far_recv, norm_send, norm_recv,
      ag_send, ag_recv, sib_send, sib_recv, out_sem, vload_sem, vsend_sem, vrecv_sem, vout_sem) = refs[36:]
     chips = replicas // CORES
@@ -107,34 +124,49 @@
     def step_rows(i):
         return 64 if AXES[i] == 0 else 32
 
-    def each(i, body, init=None):
-        rows = length if AXES[i] == 0 else width
+    def half(i):
+        return (length if AXES[i] == 0 else width) // 2
+
+    def each(i, body, init=None, parts=(0, 1)):
         step = step_rows(i)
 
         def run(j, carry):
             return body(pl.ds(pl.multiple_of(j * step, step), step), carry)
 
-        return lax.fori_loop(0, rows // step, run, init)
+        start, stop = parts[0] * half(i), (parts[-1] + 1) * half(i)
+        return lax.fori_loop(start // step, stop // step, run, init)
 
     def add_sibling(i, d):
         loads[i, d].wait()
         near[i, d].wait_recv()
         own, sib = at(own_r, own_c, i, d), at(sib_r, sib_c, i, d)
-
-        def body(rows, carry):
+        code = at(code_r, code_c, i, d - 1) if d > 0 else None
+
+        def whole(rows, carry):
             own[rows, :] = own[rows, :] + sib[rows, :]
             return carry
 
-        each(i, body, 0)
+        def coded(rows, carry):
+            code[rows, :] = encode(own[rows, :] + sib[rows, :])
+            return carry
+
+        if d > 0:
+            each(i, coded, 0, (0,))
+            each(i, whole, 0, (1,))
+        else:
+            each(i, whole, 0)
 
     far = {}
     for i in range(n):
         for d in range(1, chips):
             add_sibling(i, d)
-            far[i, d] = remote(
-                at(own_r, own_c, i, d), at(rem_r, rem_c, i, d - 1), far_send.at[i, d - 1], far_recv.at[i, d - 1],
-                to_replica(chip_at(d) * CORES + core))
-            far[i, d].start()
+            lower = pl.ds(half(i), half(i))
+            for k, (src, dst) in enumerate((
+                    (at(code_r, code_c, i, d - 1), at(rem_r, rem_c, i, d - 1)),
+                    (at(own_r, own_c, i, d).at[lower, :], at(full_r, full_c, i, d - 1)))):
+                far[i, d, k] = remote(src, dst, far_send.at[i, d - 1, k], far_recv.at[i, d - 1, k],
+                                      to_replica(chip_at(d) * CORES + core))
+                far[i, d, k].start()
 
     lanes = lax.broadcasted_iota(jnp.int32, (64, 128), 1)
     for i in range(n):
@@ -167,8 +199,7 @@
         stepped, state = update(total * rate, vfull[k], vfull[2 + k])
         vfull[k] = stepped
         vfull[2 + k] = state
-        vcomp[k] = stepped.astype(jnp.bfloat16)
-        vouts.append(pltpu.make_async_copy(vcomp.at[k], vec_compute[k], vout_sem.at[k]))
+        vouts.append(pltpu.make_async_copy(vfull.at[k], vec_compute[k], vout_sem.at[k]))
         vouts.append(pltpu.make_async_copy(vfull.at[k, :, mine], vec_stepped[k], vout_sem.at[2 + k]))
         vouts.append(pltpu.make_async_copy(vfull.at[2 + k, :, mine], vec_state[k], vout_sem.at[4 + k]))
     for c in vouts:
@@ -179,15 +210,32 @@
     gather, give = {}, {}
     for i in range(n):
         for d in range(1, chips):
-            far[i, d].wait_recv()
+            far[i, d, 0].wait_recv()
+            far[i, d, 1].wait_recv()
         own = at(own_r, own_c, i, 0)
         rem = [at(rem_r, rem_c, i, d) for d in range(chips - 1)]
-
-        def mean_of(rows, own=own, rem=rem):
+        full = [at(full_r, full_c, i, d) for d in range(chips - 1)]
+
+        def add_coded(rows, carry, own=own, rem=rem):
             total = own[rows, :]
             for r in rem:
-                total = total + r[rows, :]
-            total = total * rate
+                total = total + decode(r[rows, :])
+            own[rows, :] = total
+            return carry
+
+        def add_full(rows, carry, own=own, full=full, i=i):
+            there = pl.ds(pl.multiple_of(rows.start - half(i), step_rows(i)), step_rows(i))
+            total = own[rows, :]
+            for r in full:
+                total = total + r[there, :]
+            own[rows, :] = total
+            return carry
+
+        each(i, add_coded, 0, (0,))
+        each(i, add_full, 0, (1,))
+
+        def mean_of(rows, own=own):
+            total = own[rows, :] * rate
             own[rows, :] = total
             return total
 
@@ -274,6 +322,20 @@
         c.wait()
 
 
+def write_out(count, *refs):
+    source, target, held = refs[:count], refs[count:2 * count], refs[2 * count:3 * count]
+    in_sem, out_sem = refs[3 * count:]
+    reads = [pltpu.make_async_copy(a, b, in_sem.at[k]) for k, (a, b) in enumerate(zip(source, held))]
+    writes = [pltpu.make_async_copy(a, b, out_sem.at[k]) for k, (a, b) in enumerate(zip(held, target))]
+    for c in reads:
+        c.start()
+    for read, c in zip(reads, writes):
+        read.wait()
+        c.start()
+    for c in writes:
+        c.wait()
+
+
 def shards(*args):
     replicas, models = lax.axis_size("replica"), lax.axis_size("model")
     chips = replicas // CORES
@@ -288,24 +350,24 @@
     outs = []
     for a in AXES:
         outs.append(jax.ShapeDtypeStruct((total, width) if a == 0 else (width, total), bf16))
-    outs += [jax.ShapeDtypeStruct((1, total), bf16)] * 2
+    outs += [jax.ShapeDtypeStruct((1, total), f32)] * 2
     one = [jax.ShapeDtypeStruct(row if a == 0 else col, f32) for a in AXES]
     one += [jax.ShapeDtypeStruct((1, length), f32)] * 2
     outs += one + one
     dma = pltpu.SemaphoreType.DMA
     scratch = []
-    for lead, kind in ((chips, f32), (chips, f32), (chips - 1, f32), (None, f32), (None, f32), (None, bf16),
+    for lead, kind in ((chips, f32), (chips, f32), (1 - chips, bf16), (1 - chips, bf16), (1 - chips, f32), (None, f32), (None, f32), (None, bf16),
                        (chips - 1, bf16), (chips, bf16)):
-        more = () if lead is None else (lead,)
-        scratch += [pltpu.VMEM((rows,) + more + row, kind), pltpu.VMEM(more + col, kind)]
+        more, cuts = ((), 1) if lead is None else ((abs(lead),), 2 if lead < 0 else 1)
+        scratch += [pltpu.VMEM((rows,) + more + (length // cuts, width), kind),
+                    pltpu.VMEM(more + (width // cuts, length), kind)]
     scratch += [
         pltpu.VMEM((rows, length, 128), f32),
         pltpu.VMEM((rows, length, 128), f32),
         pltpu.VMEM((n, models, 8, length), f32),
         pltpu.VMEM((2, replicas, 1, total), f32),
         pltpu.VMEM((4, 1, total), f32),
-        pltpu.VMEM((2, 1, total), bf16),
-        dma((n, chips + 2)), dma((n, chips)), dma((n, chips)), dma((n, chips - 1)), dma((n, chips - 1)),
+        dma((n, chips + 2)), dma((n, chips)), dma((n, chips)), dma((n, chips - 1, 2)), dma((n, chips - 1, 2)),
         dma((n, models - 1)), dma((n, models - 1)),
         dma((n, chips - 1)), dma((n, chips - 1)), dma((n, chips)), dma((n, chips)),
         dma((n, 2 + 2 * chips)), dma((6,)), dma((replicas - 1, 6)), dma((replicas - 1, 6)), dma((6,)),
@@ -320,8 +382,21 @@
         compiler_params=pltpu.CompilerParams(collective_id=0, has_side_effects=True),
     )(*args)
     result = list(result)
+    picks = [k for k in range(len(outs)) if k not in (4, 5)][::-1]
+    shapes = [outs[k] for k in picks]
+    placed = pl.pallas_call(
+        functools.partial(write_out, len(picks)),
+        out_shape=shapes,
+        in_specs=[anywhere] * len(picks),
+        out_specs=[anywhere] * len(picks),
+        scratch_shapes=[pltpu.VMEM(a.shape, a.dtype) for a in shapes] + [dma((len(picks),)), dma((len(picks),))],
+    )(*[result[k] for k in picks])
+    for k, a in zip(picks, placed):
+        result[k] = a
     for k in (4, 5, 10, 11, 16, 17):
         result[k] = result[k].reshape(-1)
+    for k in (4, 5):
+        result[k] = result[k].astype(bf16)
     return tuple(result)
 
 

time: 98.9 us -> 78.3 us (0.79)
  local copies, waits for them, and re-layouts: 14 us -> 0.01 us
  Pallas kernels: 81.2 us -> 76.8 us
  other arithmetic: 2.72 us -> 0.64 us
    unnamed x46 -> x4, local copies, waits for them, and re-layouts: 14 us -> 0.01 us
    pallas_call x1, Pallas kernels: 81.2 us -> 70.1 us  [shards(): pl.pallas_call(functools.partial(kernel, replicas, models, length, width)...]
    pallas_call x0 -> x1, Pallas kernels: none -> 6.65 us  [shards(): pl.pallas_call(functools.partial(write_out, len(picks)), out_shape=shapes...]
    pallas_call x2 -> x0, other arithmetic: 2.72 us -> none  [shards(): pl.pallas_call(functools.partial(kernel, replicas, models, length, width)...]
where the time goes in v2:
time: 78.3 us; the launch traced here: 78.1 us
  Pallas kernels  76.8 us (98%)
    pallas_call x1, Pallas kernels, shards(): pl.pallas_call(functools.partial(kernel, replicas, models, length, width)...  70.1 us
    pallas_call x1, Pallas kernels, shards(): pl.pallas_call(functools.partial(write_out, len(picks)), out_shape=shapes...  6.65 us

profile of v2, /device:TPU:0, one launch (start us, length us, event | category | flops | bytes accessed | tf_op | source)
XLA Modules:
  0.0 78.1 jit_solution(11376090434242897726)
XLA Ops:
  0.7 70.1 %shard_map.313 = (bf16[2048,256]{1,0:T(8,128)(2,1)}, bf16[2048,256]{1,0:T(8,128)(2,1)}, bf16[2048,256]{1,0:T(8,128)(2,1)}, bf16[256,2048]{1,0:T(8,128)(2,1)}, f3...) custom-call(f32[1,2048,256]{2,1,0:T(8,128)} %refs_0_.1, ...), custom_call_target="tpu_custom_call" | custom-call | tf_op jit(solution)/shard_map/pallas_call | solution.py:376
  70.8 0.0 copy-start
  70.8 0.0 copy-start.1
  70.8 6.7 %shard_map.314 = (f32[1,512]{1,0:T(1,128)}, f32[1,512]{1,0:T(1,128)}, f32[256,512]{1,0:T(8,128)}, f32[512,256]{1,0:T(8,128)}, f32[512,256]{1,0:T(8,128)}, /*inde...) custom-call(f32[1,512]{1,0:T(1,128)} %get-tuple-element.52.refs_0_, ...), custom_call_target="tpu_custom_call" | custom-call | tf_op jit(solution)/shard_map/pallas_call | solution.py:387
  77.5 0.0 copy-done
  77.5 0.0 copy-done.1
  77.5 0.6 convert_reduce_fusion
Async XLA Ops:
  70.8 6.7 %copy-start = (f32[1,2048]{1,0:T(1,128)S(1)}, f32[1,2048]{1,0:T(1,128)}, u32[]{:S(2)}) copy-start(f32[1,2048]{1,0:T(1,128)} %get-tuple-element.72) | copy-start | bytes 24580
  70.8 6.7 %copy-start.1 = (f32[1,2048]{1,0:T(1,128)S(1)}, f32[1,2048]{1,0:T(1,128)}, u32[]{:S(2)}) copy-start(f32[1,2048]{1,0:T(1,128)} %get-tuple-element.73) | copy-start | bytes 24580
